TPU v7x, 32 devices: a whole 2x2x4 slice. The times are simulated.
32 devices in a mesh: chan: 8 (over z, core), band: 4 (over y, x).
Axes of the slice: x: 2, y: 2, z: 4, core: 2. Of those that a mesh axis runs over, the one named last changes fastest.
Arguments:
- residual: float32 [64, 96, 16384], P('chan', 'band'), may hold values from -60 to 60
- weight_index: int32 [64], P('chan'), may hold values from 0 to 15
- weight_table: float32 [16], replicated, may hold values from 0.2 to 5
- gridded: float32 [2, 8, 128, 16384], P(None, 'chan', 'band'), may hold values from -6 to 6
Outputs:
- components: float32 [3, 96, 16384], P(None, 'band', 'chan')
- spectrum: float32 [2, 8, 16384, 128], P(None, 'chan', 'band')
All inputs are finite; a program needn't handle non-finite values.
Results may differ from a plain program's by a relative error of at most 0.0002.
Values sent between devices are 32-bit elements; how exact they have to be, the bound alone decides.
A program may use at most 128 MiB of HBM per device.

v0:
```python
import functools
import math

import jax
import jax.numpy as jnp
import numpy as np
from jax import lax
from jax.experimental import pallas as pl
from jax.experimental.pallas import tpu as pltpu
from jax.sharding import PartitionSpec as P

MESH = pl.DeviceIdType.MESH
LANES = 128
SUB = 8


def block_form(table):
    real = np.block([[table.real, -table.imag], [table.imag, table.real]]).astype(np.float32)
    high = real.astype(jnp.bfloat16)
    low = (real - high.astype(np.float32)).astype(jnp.bfloat16)
    return np.concatenate([high, low, high], axis=1)


def dft(size):
    grid = np.outer(np.arange(size), np.arange(size)) % size
    return np.exp(-2j * np.pi * grid / size)


def tables(length):
    outer = length // LANES
    turn = np.exp(-2j * np.pi * np.outer(np.arange(outer), np.arange(LANES)) / length)
    turn = turn / math.sqrt(length)
    return (
        block_form(dft(outer)),
        block_form(dft(LANES)),
        turn.real.astype(np.float32),
        turn.imag.astype(np.float32),
    )


def solve_terms(moment, taylor):
    s0, s1, s2, s3, s4 = (moment[j, 0] for j in range(5))
    aa = s2 * s4 - s3 * s3
    ab = s2 * s3 - s1 * s4
    ac = s1 * s3 - s2 * s2
    bb = s0 * s4 - s2 * s2
    bc = s1 * s2 - s0 * s3
    cc = s0 * s2 - s1 * s1
    determ = s0 * aa + s1 * ab + s2 * ac
    rows = ((aa, ab, ac), (ab, bb, bc), (ac, bc, cc))
    return jnp.stack(
        [sum((entry / determ) * taylor[s] for s, entry in enumerate(row)) for row in rows]
    )


def exchange_kernel(
    nc,
    nb,
    idx_ref,
    tab_ref,
    first_ref,
    second_ref,
    turn_re_ref,
    turn_im_ref,
    res_hbm,
    grid_hbm,
    spec_hbm,
    tay_ref,
    mom_ref,
    grid_v,
    out_v,
    res_v,
    part_v,
    mom_own,
    mom_all,
    *rest,
):
    steps = int(math.log2(nc))
    lands = rest[:steps]
    (grid_sem, res_sem, own_sem, fs_sem, fr_sem, rs_sem, rr_sem, ms_sem, mr_sem) = rest[steps:]
    chan = lax.axis_index("chan")
    band = lax.axis_index("band")
    tiles, outer8 = grid_v.shape[1], grid_v.shape[2]
    outer = outer8 // SUB
    rows = tiles * SUB
    kept = LANES // nb
    parts = res_v.shape[0]
    count = res_v.shape[1]
    wide = part_v.shape[3]

    def grid_copy(t):
        return pltpu.make_async_copy(grid_hbm.at[:, t], grid_v.at[:, t], grid_sem.at[t])

    def res_copy(c):
        return pltpu.make_async_copy(
            res_hbm.at[:, pl.ds(c * SUB, SUB), :], res_v.at[c], res_sem.at[c]
        )

    order = max(tiles, parts)
    for i in range(order):
        if i < tiles:
            grid_copy(i).start()
        if i < parts:
            res_copy(i).start()

    barrier = pltpu.get_barrier_semaphore()
    for d in range(1, nc):
        peer = lax.rem(chan + d, nc)
        pl.semaphore_signal(barrier, inc=1, device_id=(peer, band), device_id_type=MESH)
    for d in range(1, nb):
        peer = lax.rem(band + d, nb)
        pl.semaphore_signal(barrier, inc=1, device_id=(chan, peer), device_id_type=MESH)

    total = count * nc
    coeffs = []
    moments = [jnp.float32(0.0)] * 5
    for c in range(count):
        weight = tab_ref[idx_ref[c]]
        position = (chan * count + c).astype(jnp.float32)
        offset = (2.0 * position + 1.0) * (1.0 / total) - 1.0
        power = weight
        trio = []
        for j in range(5):
            if j < 3:
                trio.append(power)
            moments[j] = moments[j] + power
            power = power * offset
        coeffs.append(trio)
    line = lax.broadcasted_iota(jnp.int32, (SUB, LANES), 0)
    tile = jnp.zeros((SUB, LANES), jnp.float32)
    for j in range(5):
        tile = jnp.where(line == j, moments[j], tile)
    mom_own[...] = tile

    def transform(t):
        def pair(i, carry):
            cols = []
            for k in range(2):
                r = i * 2 + k
                cols.append(
                    jnp.concatenate(
                        [grid_v[p, t, pl.ds(r, outer, stride=SUB), :] for p in range(2)], axis=0
                    )
                )
            x = jnp.concatenate(cols, axis=1)
            high = x.astype(jnp.bfloat16)
            low = (x - high.astype(jnp.float32)).astype(jnp.bfloat16)
            mid = jnp.dot(
                first_ref[...],
                jnp.concatenate([high, high, low], axis=0),
                preferred_element_type=jnp.float32,
            )
            turn_re, turn_im = turn_re_ref[...], turn_im_ref[...]
            turned = []
            for k in range(2):
                re = mid[:outer, k * LANES : (k + 1) * LANES]
                im = mid[outer:, k * LANES : (k + 1) * LANES]
                turned.append(
                    jnp.concatenate(
                        [re * turn_re - im * turn_im, re * turn_im + im * turn_re], axis=1
                    )
                )
            y = jnp.concatenate(turned, axis=0)
            high = y.astype(jnp.bfloat16)
            low = (y - high.astype(jnp.float32)).astype(jnp.bfloat16)
            out = lax.dot_general(
                second_ref[...],
                jnp.concatenate([high, high, low], axis=1),
                (((1,), (1,)), ((), ())),
                preferred_element_type=jnp.float32,
            )
            for k in range(2):
                for p in range(2):
                    out_v[p, t * SUB + i * 2 + k] = out[
                        p * LANES : (p + 1) * LANES, k * outer : (k + 1) * outer
                    ]
            return carry

        lax.fori_loop(0, SUB // 2, pair, 0)

    def block_send(t, d):
        peer = lax.rem(band + d, nb)
        return pltpu.make_async_remote_copy(
            src_ref=out_v.at[:, pl.ds(t * SUB, SUB), pl.ds(peer * kept, kept), :],
            dst_ref=spec_hbm.at[:, pl.ds(band * rows + t * SUB, SUB), :, :],
            send_sem=fs_sem.at[t, d - 1],
            recv_sem=fr_sem.at[t, d - 1],
            device_id=(chan, peer),
            device_id_type=MESH,
        )

    def block_keep(t):
        return pltpu.make_async_copy(
            out_v.at[:, pl.ds(t * SUB, SUB), pl.ds(band * kept, kept), :],
            spec_hbm.at[:, pl.ds(band * rows + t * SUB, SUB), :, :],
            own_sem.at[t],
        )

    def weigh(c):
        step = 512 if wide % 512 == 0 else LANES

        def one(j, carry):
            spot = 0
            for s in range(steps):
                spot = spot + ((j // (1 << s)) % 2) * (1 << (steps - 1 - s))
            for q in range(wide // step):
                col = pl.multiple_of(j * wide + q * step, LANES)
                sums = [None] * 3
                for ch in range(count):
                    x = res_v[c, ch, :, pl.ds(col, step)]
                    for t in range(3):
                        term = coeffs[ch][t] * x
                        sums[t] = term if ch == 0 else sums[t] + term
                for t in range(3):
                    part_v[c, spot, pl.ds(t * SUB, SUB), pl.ds(q * step, step)] = sums[t]
            return carry

        lax.fori_loop(0, nc, one, 0)

    bits = [(chan // (1 << s)) % 2 for s in range(steps)]
    partners = [chan + (1 - 2 * bits[s]) * (1 << s) for s in range(steps)]
    starts = [0]
    for s in range(steps):
        starts.append(starts[s] + bits[s] * (nc >> (s + 1)))

    def half_send(c, s):
        size = nc >> (s + 1)
        begin = starts[s] + (1 - bits[s]) * size
        return pltpu.make_async_remote_copy(
            src_ref=part_v.at[c, pl.ds(begin, size)],
            dst_ref=lands[s].at[c],
            send_sem=rs_sem.at[c, s],
            recv_sem=rr_sem.at[c, s],
            device_id=(partners[s], band),
            device_id_type=MESH,
        )

    def half_add(c, s):
        half_send(c, s).wait_recv()
        size = nc >> (s + 1)
        if s == steps - 1:
            for t in range(3):
                span = pl.ds(t * SUB, SUB)
                tay_ref[t, c] = part_v[c, starts[s + 1], span, :] + lands[s][c, 0, span, :]
            return
        half = size // 2
        for mine in (1 - bits[s + 1], bits[s + 1]):
            for q in range(half):
                at = mine * half + q
                part_v[c, starts[s + 1] + at] = part_v[c, starts[s + 1] + at] + lands[s][c, at]
            if mine is not bits[s + 1]:
                half_send(c, s + 1).start()

    def mom_send(d):
        peer = lax.rem(chan + d, nc)
        return pltpu.make_async_remote_copy(
            src_ref=mom_own,
            dst_ref=mom_all.at[d - 1],
            send_sem=ms_sem.at[d - 1],
            recv_sem=mr_sem.at[d - 1],
            device_id=(peer, band),
            device_id_type=MESH,
        )

    for i in range(order):
        if i < tiles:
            grid_copy(i).wait()
            transform(i)
            if i == 0:
                pl.semaphore_wait(barrier, nc + nb - 2)
            for d in range(1, nb):
                block_send(i, d).start()
            block_keep(i).start()
        if i < parts:
            res_copy(i).wait()
            weigh(i)
            half_send(i, 0).start()
        if 1 <= i <= parts:
            half_add(i - 1, 0)
    if parts >= order:
        half_add(parts - 1, 0)
    for d in range(1, nc):
        mom_send(d).start()
    for s in range(1, steps):
        for c in range(parts):
            half_add(c, s)
    moment = mom_own[...]
    for d in range(1, nc):
        mom_send(d).wait_recv()
        moment = moment + mom_all[d - 1]
    mom_ref[...] = moment
    for d in range(1, nc):
        mom_send(d).wait_send()
    for c in range(parts):
        for s in range(steps):
            half_send(c, s).wait_send()
    for t in range(tiles):
        block_keep(t).wait()
        for d in range(1, nb):
            block_send(t, d).wait()


def turn_kernel(in_ref, out_ref):
    many, outer = in_ref.shape[2], in_ref.shape[3]
    for k in range(many):
        out_ref[0, 0, pl.ds(k * outer, outer), :] = in_ref[0, :, k, :].T


def local(nc, nb, residual, weight_index, weight_table, gridded):
    count, row_count, columns = residual.shape
    _, groups, rows, length = gridded.shape
    outer = length // LANES
    tiles, parts = rows // SUB, row_count // SUB
    wide = columns // nc
    kept = LANES // nb
    steps = int(math.log2(nc))
    view = gridded.reshape(2, tiles, SUB, outer, LANES)
    view = jnp.transpose(view, (0, 1, 3, 2, 4)).reshape(2, tiles, outer * SUB, LANES)
    vmem = pl.BlockSpec(memory_space=pltpu.VMEM)
    smem = pl.BlockSpec(memory_space=pltpu.SMEM)
    hbm = pl.BlockSpec(memory_space=pl.ANY)
    dma = pltpu.SemaphoreType.DMA
    raw, taylor, moment = pl.pallas_call(
        functools.partial(exchange_kernel, nc, nb),
        out_shape=(
            jax.ShapeDtypeStruct((2, nb * rows, kept, outer), jnp.float32),
            jax.ShapeDtypeStruct((3, parts, SUB, wide), jnp.float32),
            jax.ShapeDtypeStruct((SUB, LANES), jnp.float32),
        ),
        in_specs=[smem, smem, vmem, vmem, vmem, vmem, hbm, hbm],
        out_specs=(hbm, vmem, vmem),
        scratch_shapes=[
            pltpu.VMEM((2, tiles, outer * SUB, LANES), jnp.float32),
            pltpu.VMEM((2, rows, LANES, outer), jnp.float32),
            pltpu.VMEM((parts, count, SUB, columns), jnp.float32),
            pltpu.VMEM((parts, nc, 3 * SUB, wide), jnp.float32),
            pltpu.VMEM((SUB, LANES), jnp.float32),
            pltpu.VMEM((nc - 1, SUB, LANES), jnp.float32),
            *[
                pltpu.VMEM((parts, nc >> (s + 1), 3 * SUB, wide), jnp.float32)
                for s in range(steps)
            ],
            dma((tiles,)),
            dma((parts,)),
            dma((tiles,)),
            dma((tiles, nb - 1)),
            dma((tiles, nb - 1)),
            dma((parts, steps)),
            dma((parts, steps)),
            dma((nc - 1,)),
            dma((nc - 1,)),
        ],
        compiler_params=pltpu.CompilerParams(
            collective_id=0, has_side_effects=True, vmem_limit_bytes=60 * 1024 * 1024
        ),
        name="exchange",
    )(weight_index, weight_table, *map(jnp.asarray, tables(length)), residual, view)
    many = min(SUB, kept)
    spectrum = pl.pallas_call(
        turn_kernel,
        grid=(2, kept // many),
        out_shape=jax.ShapeDtypeStruct((2, 1, kept * outer, nb * rows), jnp.float32),
        in_specs=[pl.BlockSpec((1, nb * rows, many, outer), lambda p, k: (p, 0, k, 0))],
        out_specs=pl.BlockSpec((1, 1, many * outer, nb * rows), lambda p, k: (p, 0, k, 0)),
        name="turn",
    )(raw)
    components = solve_terms(moment, taylor.reshape(3, row_count, wide))
    return (components, spectrum)


def solution(mesh):
    nc, nb = mesh.shape["chan"], mesh.shape["band"]
    in_specs = (P("chan", "band", None), P("chan"), P(), P(None, "chan", "band", None))
    out_specs = (P(None, "band", "chan"), P(None, "chan", "band", None))
    return jax.shard_map(
        functools.partial(local, nc, nb),
        mesh=mesh,
        in_specs=in_specs,
        out_specs=out_specs,
        check_vma=False,
    )
```

profile of v0, /device:TPU:0, one launch (start us, length us, event | category | flops | bytes accessed | tf_op | source)
XLA Modules:
  0.0 87.7 jit_solution(6275192956066318708)
XLA Ops:
  0.6 59.9 %exchange.1 = (f32[2,128,32,128]{3,2,1,0:T(8,128)}, f32[3,3,8,2048]{3,2,1,0:T(8,128)}, f32[8,128]{1,0:T(8,128)}) custom-call(s32[8]{0:T(128)} %idx_ref.1, f32[16]{0:T(128)} %tab_ref.1, bf16[256,768]{1,0:T(8,128)(2,1)} %constant.6.clone.first_ref.second_ref, bf16[256,768]{1,0:T(8,128)(2,1)} %constant.6.clone.first_ref.second_ref, ...), custom_call_target="tpu_custom_call" | custom-call | tf_op jit(solution)/shard_map/exchange/pallas_call | solution.py:323
  60.5 1.5 %fusion = (f32[1,1]{1,0:T(1,128)}, f32[1,1]{1,0:T(1,128)}, f32[1,1]{1,0:T(1,128)}, f32[1,1]{1,0:T(1,128)}, f32[1,1]{1,0:T(1,128)}) fusion(f32[8,128]{1,0:T(8,128)} %get-tuple-element.5), kind=kLoop, calls=%fused_computation.4 | loop fusion | bytes 40 | tf_op jit(solution)/shard_map/slice | solution.py:42
  77.9 1.2 %add_bitcast_fusion.2 = (f32[1,24,2048]{2,1,0:T(8,128)S(1)}, f32[1,24,2048]{2,1,0:T(8,128)S(1)}, f32[1,24,2048]{2,1,0:T(8,128)S(1)}) fusion(f32[3,3,8,2048]{3,2,1,0:T(8,128)} %get-tuple-element.6, f32[]{:T(128)S(6)} %div.23, f32[]{:T(128)S(6)} %div.22, f32[]{:T(128)S(6)} %div.21, f32[]{:T(128)S(6)} %div.25, f32[]{:T(128)S(6)} %div.24, f32[]{:T(128)S(6)} %div.26), kind=kLoop, calls=%fused_computation.3 | loop fusion | flops 737280 | bytes 1179672 | tf_op jit(solution)/shard_map/add | solution.py:52
  79.2 0.9 pad_maximum_fusion
  80.0 7.6 %turn.1 = f32[2,1,4096,128]{3,2,1,0:T(8,128)} custom-call(f32[2,128,32,128]{3,2,1,0:T(8,128)} %get-tuple-element.7.in_ref), custom_call_target="tpu_custom_call" | custom-call | tf_op jit(solution)/shard_map/turn/pallas_call | solution.py:359
where the time goes:
time: 88.2 us; the launch traced here: 87.7 us
  Pallas kernels  67.5 us (77%)
  between operations  16.6 us (19%)
  other arithmetic  2.08 us (2%)
  local copies, waits for them, and re-layouts  1.47 us (2%)
    pallas_call x1, Pallas kernels, local(): pl.pallas_call(functools.partial(exchange_kernel, nc, nb), out_shape=(jax...  59.9 us
    pallas_call x1, Pallas kernels, local(): pl.pallas_call(turn_kernel, grid=(2, kept // many), out_shape=jax.ShapeDt...  7.64 us

commit v1 on v0

--- a/solution.py
+++ b/solution.py
@@ -38,8 +38,8 @@
     )
 
 
-def solve_terms(moment, taylor):
-    s0, s1, s2, s3, s4 = (moment[j, 0] for j in range(5))
+def inverse_rows(moment):
+    s0, s1, s2, s3, s4 = (moment[j : j + 1, :] for j in range(5))
     aa = s2 * s4 - s3 * s3
     ab = s2 * s3 - s1 * s4
     ac = s1 * s3 - s2 * s2
@@ -47,10 +47,7 @@
     bc = s1 * s2 - s0 * s3
     cc = s0 * s2 - s1 * s1
     determ = s0 * aa + s1 * ab + s2 * ac
-    rows = ((aa, ab, ac), (ab, bb, bc), (ac, bc, cc))
-    return jnp.stack(
-        [sum((entry / determ) * taylor[s] for s, entry in enumerate(row)) for row in rows]
-    )
+    return [entry / determ for entry in (aa, ab, ac, bb, bc, cc)]
 
 
 def exchange_kernel(
@@ -288,7 +285,11 @@
     for d in range(1, nc):
         mom_send(d).wait_recv()
         moment = moment + mom_all[d - 1]
-    mom_ref[...] = moment
+    entries = inverse_rows(moment)
+    result = jnp.zeros((SUB, LANES), jnp.float32)
+    for j, entry in enumerate(entries):
+        result = jnp.where(line == j, entry, result)
+    mom_ref[...] = result
     for d in range(1, nc):
         mom_send(d).wait_send()
     for c in range(parts):
@@ -300,10 +301,13 @@
             block_send(t, d).wait()
 
 
-def turn_kernel(in_ref, out_ref):
+def turn_kernel(inv_ref, in_ref, tay_ref, out_ref, comp_ref):
     many, outer = in_ref.shape[2], in_ref.shape[3]
     for k in range(many):
         out_ref[0, 0, pl.ds(k * outer, outer), :] = in_ref[0, :, k, :].T
+    aa, ab, ac, bb, bc, cc = (inv_ref[j, 0] for j in range(6))
+    for t, row in enumerate(((aa, ab, ac), (ab, bb, bc), (ac, bc, cc))):
+        comp_ref[t] = row[0] * tay_ref[0] + row[1] * tay_ref[1] + row[2] * tay_ref[2]
 
 
 def local(nc, nb, residual, weight_index, weight_table, gridded):
@@ -356,15 +360,28 @@
         name="exchange",
     )(weight_index, weight_table, *map(jnp.asarray, tables(length)), residual, view)
     many = min(SUB, kept)
-    spectrum = pl.pallas_call(
+    cuts = 2 * (kept // many)
+    piece = pl.BlockSpec(
+        (3, row_count, wide // cuts), lambda p, k: (0, 0, p * (kept // many) + k)
+    )
+    spectrum, components = pl.pallas_call(
         turn_kernel,
         grid=(2, kept // many),
-        out_shape=jax.ShapeDtypeStruct((2, 1, kept * outer, nb * rows), jnp.float32),
-        in_specs=[pl.BlockSpec((1, nb * rows, many, outer), lambda p, k: (p, 0, k, 0))],
-        out_specs=pl.BlockSpec((1, 1, many * outer, nb * rows), lambda p, k: (p, 0, k, 0)),
+        out_shape=(
+            jax.ShapeDtypeStruct((2, 1, kept * outer, nb * rows), jnp.float32),
+            jax.ShapeDtypeStruct((3, row_count, wide), jnp.float32),
+        ),
+        in_specs=[
+            smem,
+            pl.BlockSpec((1, nb * rows, many, outer), lambda p, k: (p, 0, k, 0)),
+            piece,
+        ],
+        out_specs=(
+            pl.BlockSpec((1, 1, many * outer, nb * rows), lambda p, k: (p, 0, k, 0)),
+            piece,
+        ),
         name="turn",
-    )(raw)
-    components = solve_terms(moment, taylor.reshape(3, row_count, wide))
+    )(moment, raw, taylor.reshape(3, row_count, wide))
     return (components, spectrum)
 
 

time: 88.2 us -> 68.6 us (0.78)
  between operations: 16.6 us -> 0.64 us
  other arithmetic: 2.08 us -> 0 us
  local copies, waits for them, and re-layouts: 1.47 us -> 0 us
    slice x1 -> x0, local copies, waits for them, and re-layouts: 1.47 us -> none  [solve_terms(): s0, s1, s2, s3, s4 = (moment[j, 0] for j in range(5))]
    add x1 -> x0, other arithmetic: 1.22 us -> none  [solve_terms(): sum((entry / determ * taylor[s] for s, entry in enumerate(row)))]
where the time goes in v1:
time: 68.6 us; the launch traced here: 68.3 us
  Pallas kernels  67.7 us (99%)
    pallas_call x1, Pallas kernels, local(): pl.pallas_call(functools.partial(exchange_kernel, nc, nb), out_shape=(jax...  59.9 us
    pallas_call x1, Pallas kernels, local(): pl.pallas_call(turn_kernel, grid=(2, kept // many), out_shape=(jax.ShapeD...  7.78 us

profile of v1, /device:TPU:0, one launch (start us, length us, event | category | flops | bytes accessed | tf_op | source)
XLA Modules:
  0.0 68.3 jit_solution(16807765384548384489)
XLA Ops:
  0.6 59.9 %exchange.1 = (f32[2,128,32,128]{3,2,1,0:T(8,128)}, f32[3,3,8,2048]{3,2,1,0:T(8,128)}, f32[8,128]{1,0:T(8,128)}) custom-call(s32[8]{0:T(128)} %idx_ref.1, f32[16]{0:T(128)} %tab_ref.1, bf16[256,768]{1,0:T(8,128)(2,1)} %constant.6.clone.first_ref.second_ref, bf16[256,768]{1,0:T(8,128)(2,1)} %constant.6.clone.first_ref.second_ref, ...), custom_call_target="tpu_custom_call" | custom-call | tf_op jit(solution)/shard_map/exchange/pallas_call | solution.py:327
  60.5 7.8 %turn.1 = (f32[2,1,4096,128]{3,2,1,0:T(8,128)}, f32[3,24,2048]{2,1,0:T(8,128)}) custom-call(f32[8,128]{1,0:T(8,128)} %get-tuple-element.7.inv_ref, f32[2,128,32,128]{3,2,1,0:T(8,128)} %get-tuple-element.8.in_ref, f32[3,24,2048]{2,1,0:T(8,128)} %bitcast.7), custom_call_target="tpu_custom_call" | custom-call | tf_op jit(solution)/shard_map/turn/pallas_call | solution.py:367

commit v2 on v1

--- a/solution.py
+++ b/solution.py
@@ -84,6 +84,8 @@
     parts = res_v.shape[0]
     count = res_v.shape[1]
     wide = part_v.shape[3]
+    chunks = part_v.shape[0]
+    cuts = chunks // parts
 
     def grid_copy(t):
         return pltpu.make_async_copy(grid_hbm.at[:, t], grid_v.at[:, t], grid_sem.at[t])
@@ -95,10 +97,10 @@
 
     order = max(tiles, parts)
     for i in range(order):
+        if i < parts:
+            res_copy(i).start()
         if i < tiles:
             grid_copy(i).start()
-        if i < parts:
-            res_copy(i).start()
 
     barrier = pltpu.get_barrier_semaphore()
     for d in range(1, nc):
@@ -201,10 +203,10 @@
             for s in range(steps):
                 spot = spot + ((j // (1 << s)) % 2) * (1 << (steps - 1 - s))
             for q in range(wide // step):
-                col = pl.multiple_of(j * wide + q * step, LANES)
+                col = pl.multiple_of((j * cuts + c % cuts) * wide + q * step, LANES)
                 sums = [None] * 3
                 for ch in range(count):
-                    x = res_v[c, ch, :, pl.ds(col, step)]
+                    x = res_v[c // cuts, ch, :, pl.ds(col, step)]
                     for t in range(3):
                         term = coeffs[ch][t] * x
                         sums[t] = term if ch == 0 else sums[t] + term
@@ -232,20 +234,20 @@
             device_id_type=MESH,
         )
 
-    def half_add(c, s):
+    def half_add(c, s, send=True):
         half_send(c, s).wait_recv()
         size = nc >> (s + 1)
         if s == steps - 1:
             for t in range(3):
                 span = pl.ds(t * SUB, SUB)
-                tay_ref[t, c] = part_v[c, starts[s + 1], span, :] + lands[s][c, 0, span, :]
+                tay_ref[t, c // cuts, :, pl.ds(c % cuts * wide, wide)] = part_v[c, starts[s + 1], span, :] + lands[s][c, 0, span, :]
             return
         half = size // 2
         for mine in (1 - bits[s + 1], bits[s + 1]):
             for q in range(half):
                 at = mine * half + q
                 part_v[c, starts[s + 1] + at] = part_v[c, starts[s + 1] + at] + lands[s][c, at]
-            if mine is not bits[s + 1]:
+            if send and mine is not bits[s + 1]:
                 half_send(c, s + 1).start()
 
     def mom_send(d):
@@ -259,27 +261,41 @@
             device_id_type=MESH,
         )
 
+    ahead = min(2, chunks)
+    moved = 0
+
+    def advance(limit):
+        nonlocal moved
+        while moved < limit:
+            half_add(moved, 1)
+            if moved + ahead < chunks:
+                half_send(moved + ahead, 1).start()
+            moved += 1
+
     for i in range(order):
+        if i < parts:
+            res_copy(i).wait()
+            for c in range(i * cuts, (i + 1) * cuts):
+                weigh(c)
+                if c == 0:
+                    pl.semaphore_wait(barrier, nc + nb - 2)
+                half_send(c, 0).start()
         if i < tiles:
             grid_copy(i).wait()
             transform(i)
-            if i == 0:
-                pl.semaphore_wait(barrier, nc + nb - 2)
             for d in range(1, nb):
                 block_send(i, d).start()
             block_keep(i).start()
         if i < parts:
-            res_copy(i).wait()
-            weigh(i)
-            half_send(i, 0).start()
-        if 1 <= i <= parts:
-            half_add(i - 1, 0)
-    if parts >= order:
-        half_add(parts - 1, 0)
+            for c in range(i * cuts, (i + 1) * cuts):
+                half_add(c, 0, send=c < ahead)
+        if i >= 1:
+            advance(min(i, (min(i + 1, parts)) * cuts - ahead))
     for d in range(1, nc):
         mom_send(d).start()
-    for s in range(1, steps):
-        for c in range(parts):
+    advance(chunks)
+    for s in range(2, steps):
+        for c in range(chunks):
             half_add(c, s)
     moment = mom_own[...]
     for d in range(1, nc):
@@ -292,7 +308,7 @@
     mom_ref[...] = result
     for d in range(1, nc):
         mom_send(d).wait_send()
-    for c in range(parts):
+    for c in range(chunks):
         for s in range(steps):
             half_send(c, s).wait_send()
     for t in range(tiles):
@@ -316,6 +332,7 @@
     outer = length // LANES
     tiles, parts = rows // SUB, row_count // SUB
     wide = columns // nc
+    halves = 2
     kept = LANES // nb
     steps = int(math.log2(nc))
     view = gridded.reshape(2, tiles, SUB, outer, LANES)
@@ -337,11 +354,11 @@
             pltpu.VMEM((2, tiles, outer * SUB, LANES), jnp.float32),
             pltpu.VMEM((2, rows, LANES, outer), jnp.float32),
             pltpu.VMEM((parts, count, SUB, columns), jnp.float32),
-            pltpu.VMEM((parts, nc, 3 * SUB, wide), jnp.float32),
+            pltpu.VMEM((parts * halves, nc, 3 * SUB, wide // halves), jnp.float32),
             pltpu.VMEM((SUB, LANES), jnp.float32),
             pltpu.VMEM((nc - 1, SUB, LANES), jnp.float32),
             *[
-                pltpu.VMEM((parts, nc >> (s + 1), 3 * SUB, wide), jnp.float32)
+                pltpu.VMEM((parts * halves, nc >> (s + 1), 3 * SUB, wide // halves), jnp.float32)
                 for s in range(steps)
             ],
             dma((tiles,)),
@@ -349,8 +366,8 @@
             dma((tiles,)),
             dma((tiles, nb - 1)),
             dma((tiles, nb - 1)),
-            dma((parts, steps)),
-            dma((parts, steps)),
+            dma((parts * halves, steps)),
+            dma((parts * halves, steps)),
             dma((nc - 1,)),
             dma((nc - 1,)),
         ],
@@ -359,7 +376,7 @@
         ),
         name="exchange",
     )(weight_index, weight_table, *map(jnp.asarray, tables(length)), residual, view)
-    many = min(SUB, kept)
+    many = min(2 * SUB, kept)
     cuts = 2 * (kept // many)
     piece = pl.BlockSpec(
         (3, row_count, wide // cuts), lambda p, k: (0, 0, p * (kept // many) + k)

time: 68.6 us -> 65.9 us (0.961)
  Pallas kernels: 67.7 us -> 65.1 us
    pallas_call x1, Pallas kernels: 7.78 us -> 6.14 us  [local(): pl.pallas_call(turn_kernel, grid=(2, kept // many), out_shape=(jax.ShapeD...]
    pallas_call x1, Pallas kernels: 59.9 us -> 58.9 us  [local(): pl.pallas_call(functools.partial(exchange_kernel, nc, nb), out_shape=(jax...]
where the time goes in v2:
time: 65.9 us; the launch traced here: 65.7 us
  Pallas kernels  65.1 us (99%)
    pallas_call x1, Pallas kernels, local(): pl.pallas_call(functools.partial(exchange_kernel, nc, nb), out_shape=(jax...  58.9 us
    pallas_call x1, Pallas kernels, local(): pl.pallas_call(turn_kernel, grid=(2, kept // many), out_shape=(jax.ShapeD...  6.14 us

profile of v2, /device:TPU:0, one launch (start us, length us, event | category | flops | bytes accessed | tf_op | source)
XLA Modules:
  0.0 65.7 jit_solution(13005988511802184106)
XLA Ops:
  0.6 58.9 %exchange.1 = (f32[2,128,32,128]{3,2,1,0:T(8,128)}, f32[3,3,8,2048]{3,2,1,0:T(8,128)}, f32[8,128]{1,0:T(8,128)}) custom-call(s32[8]{0:T(128)} %idx_ref.1, f32[16]{0:T(128)} %tab_ref.1, bf16[256,768]{1,0:T(8,128)(2,1)} %constant.6.clone.first_ref.second_ref, bf16[256,768]{1,0:T(8,128)(2,1)} %constant.6.clone.first_ref.second_ref, ...), custom_call_target="tpu_custom_call" | custom-call | tf_op jit(solution)/shard_map/exchange/pallas_call | solution.py:344
  59.6 6.1 %turn.1 = (f32[2,1,4096,128]{3,2,1,0:T(8,128)}, f32[3,24,2048]{2,1,0:T(8,128)}) custom-call(f32[8,128]{1,0:T(8,128)} %get-tuple-element.7.inv_ref, f32[2,128,32,128]{3,2,1,0:T(8,128)} %get-tuple-element.8.in_ref, f32[3,24,2048]{2,1,0:T(8,128)} %bitcast.7), custom_call_target="tpu_custom_call" | custom-call | tf_op jit(solution)/shard_map/turn/pallas_call | solution.py:384
